TPU v7x, 32 devices: a whole 2x2x4 slice. The times are simulated.
32 devices in a mesh: field: 8 (over y, x, core), slab: 4 (over z).
Axes of the slice: x: 2, y: 2, z: 4, core: 2. Of those that a mesh axis runs over, the one named last changes fastest.
Arguments:
- fields: float32 [32, 16, 16, 16, 128], P('field', None, 'slab'), may hold values from -6 to 6
- velocity: float32 [3, 16, 16, 128], P(None, 'slab'), may hold values from -0.15 to 0.15
- diffusivity: float32 [16, 16, 128], P('slab'), may hold values from 0.06 to 0.14
- noise: float32 [32, 4, 3], P('field'), may hold values from -0.8 to 0.8
- mix_rate: float32 [16, 16, 128], P('slab'), may hold values from 0.2 to 1
- evaporation: float32 [16, 16, 128], P('slab'), may hold values from 0.05 to 0.5
- rate_matrix: float32 [32, 16], replicated, may hold values from -1.5 to 1.5
- stoich: float32 [16, 32], replicated, may hold values from -1 to 1
- prefactor: float32 [32], replicated, may hold values from 0.05 to 0.5
Outputs:
- updated: float32 [32, 16, 16, 16, 128], P('field', None, 'slab')
All inputs are finite; a program needn't handle non-finite values.
Results may differ from a plain program's by a relative error of at most 0.000073.
Values sent between devices are 32-bit elements; how exact they have to be, the bound alone decides.
A program may use at most 64 MiB of HBM per device.

v0:
```python
import jax
import jax.numpy as jnp
from jax import lax
from jax.sharding import PartitionSpec as P

F = 32
SUBSTEPS = 4


def with_halo(cells, sides, width):
    for axis, dim in sides:
        count = lax.axis_size(axis)
        ends = count - 1
        head = lax.slice_in_dim(cells, 0, width, axis=dim)
        tail = lax.slice_in_dim(cells, cells.shape[dim] - width, cells.shape[dim], axis=dim)
        cells = jnp.concatenate(
            [
                lax.ppermute(tail, axis, [(i, (i + 1) % count) for i in range(ends)]),
                cells,
                lax.ppermute(head, axis, [((i + 1) % count, i) for i in range(ends)]),
            ],
            axis=dim,
        )
    return cells


def advance(padded, velocity, diffusivity, drifts):
    center = padded[:, :, 1:-1]
    x_ahead = padded[:, :, 2:]
    x_behind = padded[:, :, :-2]
    y_ahead = jnp.roll(center, -1, axis=4)
    y_behind = jnp.roll(center, 1, axis=4)
    z_ahead = jnp.roll(center, -1, axis=3)
    z_behind = jnp.roll(center, 1, axis=3)
    spread = x_ahead + x_behind + y_ahead + y_behind + z_ahead + z_behind - 6.0 * center
    stir_scale = jnp.sqrt(2.0 * diffusivity)
    drift_x = velocity[0] - stir_scale * drifts[:, 0][:, None, None, None, None]
    drift_y = velocity[1] - stir_scale * drifts[:, 1][:, None, None, None, None]
    drift_z = velocity[2] - stir_scale * drifts[:, 2][:, None, None, None, None]
    carried = (
        drift_x * (x_ahead - x_behind) * 0.5
        + drift_y * (y_ahead - y_behind) * 0.5
        + drift_z * (z_ahead - z_behind) * 0.5
    )
    return center + diffusivity * spread - carried


def react(states, average, rates, vapour, rate_matrix, stoich, prefactor):
    species = states.shape[1]
    fuel = (jnp.arange(species) == 0).astype(jnp.float32)
    mixed = states - 0.5 * rates * (states - average) + vapour * fuel[:, None]
    drive = jnp.einsum("rs,ksc->krc", rate_matrix, mixed, precision=lax.Precision.HIGHEST)
    speed = prefactor[None, :, None] * jnp.exp(2.0 * jnp.tanh(drive))
    return mixed + jnp.einsum("sr,krc->ksc", stoich, speed, precision=lax.Precision.HIGHEST)


def per_device(
    fields, velocity, diffusivity, noise, mix_rate, evaporation, rate_matrix, stoich, prefactor
):
    state = fields
    for substep in range(SUBSTEPS):
        padded = with_halo(state, (("slab", 2),), 1)
        state = advance(padded, velocity, diffusivity, noise[:, substep])
    count_fields = state.shape[0]
    species = state.shape[1]
    flattened = state.reshape(count_fields, species, -1)
    average = lax.psum(jnp.sum(flattened, axis=0), "field") / F
    reacted = react(
        flattened,
        average,
        mix_rate.reshape(-1),
        evaporation.reshape(-1),
        rate_matrix,
        stoich,
        prefactor,
    )
    return reacted.reshape(state.shape)


def solution(mesh):
    in_specs = (
        P("field", None, "slab", None, None),
        P(None, "slab", None, None),
        P("slab", None, None),
        P("field", None, None),
        P("slab", None, None),
        P("slab", None, None),
        P(),
        P(),
        P(),
    )
    out_specs = P("field", None, "slab", None, None)
    return jax.shard_map(
        per_device, mesh=mesh, in_specs=in_specs, out_specs=out_specs, check_vma=False
    )
```

profile of v0, /device:TPU:0, one launch (start us, length us, event | category | flops | bytes accessed | tf_op | source)
XLA Modules:
  0.0 167.0 jit_solution(18332196890247301672)
XLA Ops:
  6.5 2.4 %fusion.26 = (f32[4,16,1,16,128]{4,3,2,1,0:T(8,128)}, f32[4,16,1,16,128]{4,3,2,1,0:T(8,128)}) fusion(f32[4,16,4,16,128]{4,3,2,1,0:T(8,128)} %param.9), kind=kLoop, calls=%fused_computation.90 | loop fusion | bytes 2097152 | tf_op jit(solution)/shard_map/slice | solution.py:15
  10.3 5.6 %collective-permute-start.1 = (f32[4,16,1,16,128]{4,3,2,1,0:T(8,128)}, f32[4,16,1,16,128]{4,3,2,1,0:T(8,128)S(1)}, u32[]{:S(2)}, u32[]{:S(2)}) collective-permute-start(f32[4,16,1,16,128]{4,3,2,1,0:T(8,128)} %get-tuple-element.49), channel_id=1, source_target_pairs={{0,1},{1,2},{2,3},{4,5},{5,6},{6,7},{8,9},{9,10},{10,11},{12,13},{... | collective-permute-start | bytes 1572872 | tf_op jit(solution)/shard_map/ppermute | solution.py:18
  15.9 2.9 %fusion.27 = (f32[4,16,4,16,127]{4,3,2,1,0:T(8,128)}, f32[4,16,4,16,127]{4,3,2,1,0:T(8,128)}) fusion(f32[4,16,4,16,128]{4,3,2,1,0:T(8,128)S(1)} %copy-done.1), kind=kLoop, calls=%fused_computation.91 | loop fusion | bytes 8323072 | tf_op jit(solution)/shard_map/jit(_roll_static)/slice | solution.py:31
  18.8 2.9 %fusion.28 = (f32[4,16,4,16,1]{4,3,2,1,0:T(8,128)}, f32[4,16,4,16,1]{4,3,2,1,0:T(8,128)}) fusion(f32[4,16,4,16,128]{4,3,2,1,0:T(8,128)S(1)} %copy-done.1), kind=kLoop, calls=%fused_computation.92 | loop fusion | bytes 65536 | tf_op jit(solution)/shard_map/jit(_roll_static)/slice | solution.py:31
  23.7 2.3 %collective-permute-done = f32[4,16,1,16,128]{4,3,2,1,0:T(8,128)S(1)} collective-permute-done((f32[4,16,1,16,128]{4,3,2,1,0:T(8,128)}, f32[4,16,1,16,128]{4,3,2,1,0:T(8,128)S(1)}, u32[]{:S(2)}, u32[]{:S(2)}) %collective-permute-start) | collective-permute-done | bytes 524320 | tf_op jit(solution)/shard_map/ppermute | solution.py:20
  26.0 1.3 collective-permute-done.1
  27.3 2.9 %multiply_subtract_fusion.3 = f32[4,16,4,16,128]{4,3,2,1,0:T(8,128)S(1)} fusion(f32[4,16,4,16,128]{4,3,2,1,0:T(8,128)S(1)} %copy-done.1, f32[4,16,4,15,128]{4,3,2,1,0:T(8,128)S(1)} %get-tuple-element.56, f32[4,16,4,1,128]{4,3,2,1,0:T(1,128)S(1)} %get-tuple-element.58, f32[4,16,4,1,128]{4,3,2,1,0:T(1,128)S(1)} %get-tuple-element.57, ...), kind=kLoop, calls=%fused_computation.35 | loop fusion | flops 13107200 | bytes 14057472 | tf_op jit(solution)/shard_map/sub | solution.py:45
  32.1 1.3 collective-permute-start.2
  33.4 4.9 %collective-permute-start.3 = (f32[4,16,1,16,128]{4,3,2,1,0:T(8,128)S(1)}, f32[4,16,1,16,128]{4,3,2,1,0:T(8,128)S(1)}, u32[]{:S(2)}, u32[]{:S(2)}) collective-permute-start(f32[4,16,1,16,128]{4,3,2,1,0:T(8,128)S(1)} %get-tuple-element.39), channel_id=1, source_target_pairs={{0,1},{1,2},{2,3},{4,5},{5,6},{6,7},{8,9},{9,10},{10,11},{12,13},{... | collective-permute-start | bytes 1572872 | tf_op jit(solution)/shard_map/ppermute | solution.py:18
  39.2 8.2 %collective-permute-done.2 = f32[4,16,1,16,128]{4,3,2,1,0:T(8,128)S(1)} collective-permute-done((f32[4,16,1,16,128]{4,3,2,1,0:T(8,128)S(1)}, f32[4,16,1,16,128]{4,3,2,1,0:T(8,128)S(1)}, u32[]{:S(2)}, u32[]{:S(2)}) %collective-permute-start.2) | collective-permute-done | bytes 524320 | tf_op jit(solution)/shard_map/ppermute | solution.py:20
  48.6 3.0 %multiply_subtract_fusion.2 = f32[4,16,4,16,128]{4,3,2,1,0:T(8,128)S(1)} fusion(f32[4,16,4,16,128]{4,3,2,1,0:T(8,128)S(1)} %multiply_subtract_fusion.3, f32[4,16,4,15,128]{4,3,2,1,0:T(8,128)S(1)} %get-tuple-element.46, f32[4,16,4,1,128]{4,3,2,1,0:T(1,128)S(1)} %get-tuple-element.48, f32[4,16,4,1,128]{4,3,2,1,0:T(1,128)S(1)} %get-tuple-element.47, ...), kind=kLoop, calls=%fused_computation.34 | loop fusion | flops 13107200 | bytes 14057472 | tf_op jit(solution)/shard_map/sub | solution.py:45
  53.4 1.3 collective-permute-start.4
  54.7 5.2 %collective-permute-start.5 = (f32[4,16,1,16,128]{4,3,2,1,0:T(8,128)S(1)}, f32[4,16,1,16,128]{4,3,2,1,0:T(8,128)S(1)}, u32[]{:S(2)}, u32[]{:S(2)}) collective-permute-start(f32[4,16,1,16,128]{4,3,2,1,0:T(8,128)S(1)} %get-tuple-element.29), channel_id=1, source_target_pairs={{0,1},{1,2},{2,3},{4,5},{5,6},{6,7},{8,9},{9,10},{10,11},{12,13},{... | collective-permute-start | bytes 1572872 | tf_op jit(solution)/shard_map/ppermute | solution.py:18
  60.8 7.2 %collective-permute-done.4 = f32[4,16,1,16,128]{4,3,2,1,0:T(8,128)S(1)} collective-permute-done((f32[4,16,1,16,128]{4,3,2,1,0:T(8,128)S(1)}, f32[4,16,1,16,128]{4,3,2,1,0:T(8,128)S(1)}, u32[]{:S(2)}, u32[]{:S(2)}) %collective-permute-start.4) | collective-permute-done | bytes 524320 | tf_op jit(solution)/shard_map/ppermute | solution.py:20
  69.2 2.9 %multiply_subtract_fusion.1 = f32[4,16,4,16,128]{4,3,2,1,0:T(8,128)S(1)} fusion(f32[4,16,4,16,128]{4,3,2,1,0:T(8,128)S(1)} %multiply_subtract_fusion.2, f32[4,16,4,15,128]{4,3,2,1,0:T(8,128)S(1)} %get-tuple-element.36, f32[4,16,4,1,128]{4,3,2,1,0:T(1,128)S(1)} %get-tuple-element.38, f32[4,16,4,1,128]{4,3,2,1,0:T(1,128)S(1)} %get-tuple-element.37, ...), kind=kLoop, calls=%fused_computation.33 | loop fusion | flops 13107200 | bytes 14057472 | tf_op jit(solution)/shard_map/sub | solution.py:45
  73.7 1.3 collective-permute-start.6
  75.0 5.0 %collective-permute-start.7 = (f32[4,16,1,16,128]{4,3,2,1,0:T(8,128)S(1)}, f32[4,16,1,16,128]{4,3,2,1,0:T(8,128)S(1)}, u32[]{:S(2)}, u32[]{:S(2)}) collective-permute-start(f32[4,16,1,16,128]{4,3,2,1,0:T(8,128)S(1)} %get-tuple-element.20), channel_id=1, source_target_pairs={{0,1},{1,2},{2,3},{4,5},{5,6},{6,7},{8,9},{9,10},{10,11},{12,13},{... | collective-permute-start | bytes 1572872 | tf_op jit(solution)/shard_map/ppermute | solution.py:18
  80.8 6.7 %collective-permute-done.6 = f32[4,16,1,16,128]{4,3,2,1,0:T(8,128)S(1)} collective-permute-done((f32[4,16,1,16,128]{4,3,2,1,0:T(8,128)S(1)}, f32[4,16,1,16,128]{4,3,2,1,0:T(8,128)S(1)}, u32[]{:S(2)}, u32[]{:S(2)}) %collective-permute-start.6) | collective-permute-done | bytes 524320 | tf_op jit(solution)/shard_map/ppermute | solution.py:20
  88.7 3.9 %fusion.10 = (f32[16,4,16,128]{3,2,1,0:T(8,128)S(1)}, f32[4,16,4,16,128]{4,3,2,1,0:T(8,128)}) fusion(f32[4,4,16,128]{3,2,1,0:T(8,128)S(1)} %get-tuple-element.79, f32[4,4,16,128]{3,2,1,0:T(8,128)S(1)} %get-tuple-element.75, f32[4,4,16,128]{3,2,1,0:T(8,128)S(1)} %get-tuple-element.64, f32[4,16,4,16,128]{4,3,2,1,0:T(8,128)S(1)} %multiply_subtract_fusion.1, ...), kind=kLoop, calls=%fused_computation.74 | loop fusion | flops 13500416 | bytes 14581760 | tf_op jit(solution)/shard_map/reduce_sum | solution.py:67
  93.9 1.8 %reshape.150 = f32[4,16,8192]{2,1,0:T(8,128)S(1)} reshape(f32[4,16,4,16,128]{4,3,2,1,0:T(8,128)} %get-tuple-element.18) | data formatting | bytes 4194304 | tf_op jit(solution)/shard_map/reshape | solution.py:66
  95.6 54.6 %all-reduce.2.cloned.1.call-done = f32[16,8192]{1,0:T(8,128)} async-done(((f32[16,8192]{1,0:T(8,128)}), f32[16,8192]{1,0:T(8,128)}) %all-reduce.2.cloned.1.call-update) | async-done | bytes 524304 | tf_op jit(solution)/shard_map/psum | solution.py:67
  151.3 4.4 %fusion.3 = f32[4,32,8192]{2,1,0:T(8,128)S(1)} fusion(f32[32]{0:T(128)S(1)} %copy-done.12, f32[4,16,8192]{2,1,0:T(8,128)S(1)} %reshape.150, f32[16,8192]{1,0:T(8,128)S(1)} %broadcast_multiply_fusion, f32[16,8192]{1,0:T(8,128)S(1)} %broadcast_multiply_fusion.1, f32[8192]{0:T(1024)S(1)} %bitcast.39, f32[32,16]{0,1:T(8,128)S(1)} %copy-done), kind=kOutput, calls=%fused_computation.4 | convolution fusion | flops 205520896 | bytes 7374976 | tf_op jit(solution)/shard_map/rs,ksc->krc/dot_general | solution.py:52
  155.8 2.7 %fusion.4 = f32[4,16,8192]{2,1,0:T(8,128)S(1)} fusion(f32[4,32,8192]{2,1,0:T(8,128)S(1)} %fusion.3, f32[4,16,8192]{2,1,0:T(8,128)S(1)} %reshape.150, f32[16,8192]{1,0:T(8,128)S(1)} %broadcast_multiply_fusion, f32[16,8192]{1,0:T(8,128)S(1)} %broadcast_multiply_fusion.1, f32[8192]{0:T(1024)S(1)} %bitcast.40, f32[16,32]{1,0:T(8,128)S(1)} %copy-done.11), kind=kOutput, calls=%fused_computation.6 | convolution fusion | flops 203948032 | bytes 9472000 | tf_op jit(solution)/shard_map/sr,krc->ksc/dot_general | solution.py:54
  158.5 1.7 %copy.19 = f32[8,8,64,128]{3,2,1,0:T(8,128)} copy(f32[8,8,64,128]{3,1,2,0:T(8,128)S(1)} %bitcast.36) | data formatting | bytes 4194304
  (64 shorter events, 16.7 us)
Async XLA Ops:
  6.5 144.8 %copy-start = (f32[32,16]{0,1:T(8,128)S(1)}, f32[32,16]{0,1:T(8,128)}, u32[]{:S(2)}) copy-start(f32[32,16]{0,1:T(8,128)} %param.15) | copy-start | bytes 6148
  6.5 9.4 %copy-start.1 = (f32[4,16,4,16,128]{4,3,2,1,0:T(8,128)S(1)}, f32[4,16,4,16,128]{4,3,2,1,0:T(8,128)}, u32[]{:S(2)}) copy-start(f32[4,16,4,16,128]{4,3,2,1,0:T(8,128)} %param.9) | copy-start | bytes 6291460
  6.5 143.7 %all-reduce.2.cloned.1.call-start = ((), (), s32[]{:S(2)}) async-start(), calls=%async_computation | async-start | bytes 1048576 | tf_op jit(solution)/shard_map/psum | solution.py:67
  9.0 17.1 %collective-permute-start = (f32[4,16,1,16,128]{4,3,2,1,0:T(8,128)}, f32[4,16,1,16,128]{4,3,2,1,0:T(8,128)S(1)}, u32[]{:S(2)}, u32[]{:S(2)}) collective-permute-start(f32[4,16,1,16,128]{4,3,2,1,0:T(8,128)} %get-tuple-element.50), channel_id=1, source_target_pairs={{1,0},{2,1},{3,2},{5,4},{6,5},{7,6},{9,8},{10,9},{11,10},{13,12},{... | collective-permute-start | bytes 1572872 | tf_op jit(solution)/shard_map/ppermute | solution.py:20
  10.3 17.1 %collective-permute-start.1 = (f32[4,16,1,16,128]{4,3,2,1,0:T(8,128)}, f32[4,16,1,16,128]{4,3,2,1,0:T(8,128)S(1)}, u32[]{:S(2)}, u32[]{:S(2)}) collective-permute-start(f32[4,16,1,16,128]{4,3,2,1,0:T(8,128)} %get-tuple-element.49), channel_id=1, source_target_pairs={{0,1},{1,2},{2,3},{4,5},{5,6},{6,7},{8,9},{9,10},{10,11},{12,13},{... | collective-permute-start | bytes 1572872 | tf_op jit(solution)/shard_map/ppermute | solution.py:18
  18.8 2.9 %copy-start.8 = (f32[4,4,3]{1,0,2:T(4,128)S(1)}, f32[4,4,3]{1,0,2:T(4,128)}, u32[]{:S(2)}) copy-start(f32[4,4,3]{1,0,2:T(4,128)} %param.12) | copy-start | bytes 580
  18.8 3.4 %copy-start.7 = (f32[3,4,16,128]{3,2,1,0:T(8,128)S(1)}, f32[3,4,16,128]{3,2,1,0:T(8,128)}, u32[]{:S(2)}) copy-start(f32[3,4,16,128]{3,2,1,0:T(8,128)} %param.10) | copy-start | bytes 294916
  18.8 3.4 %copy-start.6 = (f32[4,16,128]{2,1,0:T(8,128)S(1)}, f32[4,16,128]{2,1,0:T(8,128)}, u32[]{:S(2)}) copy-start(f32[4,16,128]{2,1,0:T(8,128)} %param.11) | copy-start | bytes 98308
  23.1 4.2 %copy-start.2 = (f32[4,16,4,16,127]{4,3,2,1,0:T(8,128)S(1)}, f32[4,16,4,16,127]{4,3,2,1,0:T(8,128)}, u32[]{:S(2)}) copy-start(f32[4,16,4,16,127]{4,3,2,1,0:T(8,128)} %get-tuple-element.51) | copy-start | bytes 6242308
  23.1 4.2 %copy-start.3 = (f32[4,16,4,16,127]{4,3,2,1,0:T(8,128)S(1)}, f32[4,16,4,16,127]{4,3,2,1,0:T(8,128)}, u32[]{:S(2)}) copy-start(f32[4,16,4,16,127]{4,3,2,1,0:T(8,128)} %get-tuple-element.52) | copy-start | bytes 6242308
  23.2 4.2 %copy-start.4 = (f32[4,16,4,16,1]{4,3,2,1,0:T(8,128)S(1)}, f32[4,16,4,16,1]{4,3,2,1,0:T(8,128)}, u32[]{:S(2)}) copy-start(f32[4,16,4,16,1]{4,3,2,1,0:T(8,128)} %get-tuple-element.53) | copy-start | bytes 49156
  23.2 4.2 %copy-start.5 = (f32[4,16,4,16,1]{4,3,2,1,0:T(8,128)S(1)}, f32[4,16,4,16,1]{4,3,2,1,0:T(8,128)}, u32[]{:S(2)}) copy-start(f32[4,16,4,16,1]{4,3,2,1,0:T(8,128)} %get-tuple-element.54) | copy-start | bytes 49156
  32.1 15.4 %collective-permute-start.2 = (f32[4,16,1,16,128]{4,3,2,1,0:T(8,128)S(1)}, f32[4,16,1,16,128]{4,3,2,1,0:T(8,128)S(1)}, u32[]{:S(2)}, u32[]{:S(2)}) collective-permute-start(f32[4,16,1,16,128]{4,3,2,1,0:T(8,128)S(1)} %get-tuple-element.40), channel_id=1, source_target_pairs={{1,0},{2,1},{3,2},{5,4},{6,5},{7,6},{9,8},{10,9},{11,10},{13,12},{... | collective-permute-start | bytes 1572872 | tf_op jit(solution)/shard_map/ppermute | solution.py:20
  33.4 15.2 %collective-permute-start.3 = (f32[4,16,1,16,128]{4,3,2,1,0:T(8,128)S(1)}, f32[4,16,1,16,128]{4,3,2,1,0:T(8,128)S(1)}, u32[]{:S(2)}, u32[]{:S(2)}) collective-permute-start(f32[4,16,1,16,128]{4,3,2,1,0:T(8,128)S(1)} %get-tuple-element.39), channel_id=1, source_target_pairs={{0,1},{1,2},{2,3},{4,5},{5,6},{6,7},{8,9},{9,10},{10,11},{12,13},{... | collective-permute-start | bytes 1572872 | tf_op jit(solution)/shard_map/ppermute | solution.py:18
  53.4 14.6 %collective-permute-start.4 = (f32[4,16,1,16,128]{4,3,2,1,0:T(8,128)S(1)}, f32[4,16,1,16,128]{4,3,2,1,0:T(8,128)S(1)}, u32[]{:S(2)}, u32[]{:S(2)}) collective-permute-start(f32[4,16,1,16,128]{4,3,2,1,0:T(8,128)S(1)} %get-tuple-element.30), channel_id=1, source_target_pairs={{1,0},{2,1},{3,2},{5,4},{6,5},{7,6},{9,8},{10,9},{11,10},{13,12},{... | collective-permute-start | bytes 1572872 | tf_op jit(solution)/shard_map/ppermute | solution.py:20
  54.7 14.5 %collective-permute-start.5 = (f32[4,16,1,16,128]{4,3,2,1,0:T(8,128)S(1)}, f32[4,16,1,16,128]{4,3,2,1,0:T(8,128)S(1)}, u32[]{:S(2)}, u32[]{:S(2)}) collective-permute-start(f32[4,16,1,16,128]{4,3,2,1,0:T(8,128)S(1)} %get-tuple-element.29), channel_id=1, source_target_pairs={{0,1},{1,2},{2,3},{4,5},{5,6},{6,7},{8,9},{9,10},{10,11},{12,13},{... | collective-permute-start | bytes 1572872 | tf_op jit(solution)/shard_map/ppermute | solution.py:18
  73.7 13.7 %collective-permute-start.6 = (f32[4,16,1,16,128]{4,3,2,1,0:T(8,128)S(1)}, f32[4,16,1,16,128]{4,3,2,1,0:T(8,128)S(1)}, u32[]{:S(2)}, u32[]{:S(2)}) collective-permute-start(f32[4,16,1,16,128]{4,3,2,1,0:T(8,128)S(1)} %get-tuple-element.19), channel_id=1, source_target_pairs={{1,0},{2,1},{3,2},{5,4},{6,5},{7,6},{9,8},{10,9},{11,10},{13,12},{... | collective-permute-start | bytes 1572872 | tf_op jit(solution)/shard_map/ppermute | solution.py:20
  75.0 13.6 %collective-permute-start.7 = (f32[4,16,1,16,128]{4,3,2,1,0:T(8,128)S(1)}, f32[4,16,1,16,128]{4,3,2,1,0:T(8,128)S(1)}, u32[]{:S(2)}, u32[]{:S(2)}) collective-permute-start(f32[4,16,1,16,128]{4,3,2,1,0:T(8,128)S(1)} %get-tuple-element.20), channel_id=1, source_target_pairs={{0,1},{1,2},{2,3},{4,5},{5,6},{6,7},{8,9},{9,10},{10,11},{12,13},{... | collective-permute-start | bytes 1572872 | tf_op jit(solution)/shard_map/ppermute | solution.py:18
  88.7 5.0 %copy-start.9 = (f32[4,16,128]{2,1,0:T(8,128)S(1)}, f32[4,16,128]{2,1,0:T(8,128)}, u32[]{:S(2)}) copy-start(f32[4,16,128]{2,1,0:T(8,128)} %param.14) | copy-start | bytes 98308
  92.6 1.3 copy-start.10
  93.8 57.5 %copy-start.12 = (f32[32]{0:T(128)S(1)}, f32[32]{0:T(128)}, u32[]{:S(2)}) copy-start(f32[32]{0:T(128)} %param.17) | copy-start | bytes 388
  151.3 4.5 %copy-start.11 = (f32[16,32]{1,0:T(8,128)S(1)}, f32[16,32]{1,0:T(8,128)}, u32[]{:S(2)}) copy-start(f32[16,32]{1,0:T(8,128)} %param.16) | copy-start | bytes 6148
Sparse Core Ops, SparseCore 0:
  93.8 56.3 all-reduce.1
where the time goes:
time: 167 us
  waiting for transfers between devices  83.8 us (50%)
  starting transfers between devices  26 us (16%)
  local copies, waits for them, and re-layouts  22.1 us (13%)
  other arithmetic  14.2 us (9%)
  between operations  13.8 us (8%)
  matrix products  7.13 us (4%)
    psum x1, waiting for transfers between devices, per_device(): average = lax.psum(jnp.sum(flattened, axis=0), 'field') / F  54.6 us
    ppermute x4, waiting for transfers between devices, with_halo(): lax.ppermute(head, axis, [((i + 1) % count, i) for i in range(ends)])  24.4 us
    ppermute x4, starting transfers between devices, with_halo(): lax.ppermute(tail, axis, [(i, (i + 1) % count) for i in range(ends)])  20.8 us
    slice x8, local copies, waits for them, and re-layouts, advance(): y_ahead = jnp.roll(center, -1, axis=4)  10.6 us
    sub x3, other arithmetic, advance(): return center + diffusivity * spread - carried  8.86 us
    ppermute x4, starting transfers between devices, with_halo(): lax.ppermute(head, axis, [((i + 1) % count, i) for i in range(ends)])  5.16 us
    ppermute x4, waiting for transfers between devices, with_halo(): lax.ppermute(tail, axis, [(i, (i + 1) % count) for i in range(ends)])  4.83 us
    dot_general x1, matrix products, react(): jnp.einsum('rs,ksc->krc', rate_matrix, mixed, precision=lax.Precision.HIG...  4.43 us
  transfers between devices with their start and end apart: 9, of which 9 were waited for; matrix products, arithmetic and copies ran while one was open for 7% of the time, Pallas kernels for 0%

commit v1 on v0

--- a/solution.py
+++ b/solution.py
@@ -64,7 +64,7 @@
     count_fields = state.shape[0]
     species = state.shape[1]
     flattened = state.reshape(count_fields, species, -1)
-    average = lax.psum(jnp.sum(flattened, axis=0), "field") / F
+    average = jnp.sum(lax.all_gather(jnp.sum(flattened, axis=0), "field"), axis=0) / F
     reacted = react(
         flattened,
         average,

time: 167 us -> 150 us (0.90)
  waiting for transfers between devices: 83.8 us -> 65.6 us
    psum x1 -> x0, waiting for transfers between devices: 54.6 us -> none  [per_device(): average = lax.psum(jnp.sum(flattened, axis=0), 'field') / F]
    all_gather x0 -> x1, waiting for transfers between devices: none -> 36.3 us  [per_device(): lax.all_gather(jnp.sum(flattened, axis=0), 'field')]
    reduce_sum x1 -> x2, other arithmetic: 3.9 us -> 6.4 us  [the longest x1 3.94 us: per_device(): jnp.sum(flattened, axis=0)]
  transfers between devices with their start and end apart: 9 -> 9, of which waited for: 9 -> 9; matrix products, arithmetic and copies ran while one was open for 7% -> 8% of each run, Pallas kernels for 0% -> 0%
where the time goes in v1:
time: 150 us
  waiting for transfers between devices  65.6 us (44%)
  starting transfers between devices  26 us (17%)
  local copies, waits for them, and re-layouts  21.9 us (15%)
  other arithmetic  15.6 us (10%)
  between operations  13.8 us (9%)
  matrix products  7.14 us (5%)
    all_gather x1, waiting for transfers between devices, per_device(): lax.all_gather(jnp.sum(flattened, axis=0), 'field')  36.3 us
    ppermute x4, waiting for transfers between devices, with_halo(): lax.ppermute(head, axis, [((i + 1) % count, i) for i in range(ends)])  24.4 us
    ppermute x4, starting transfers between devices, with_halo(): lax.ppermute(tail, axis, [(i, (i + 1) % count) for i in range(ends)])  20.8 us
    slice x8, local copies, waits for them, and re-layouts, advance(): y_ahead = jnp.roll(center, -1, axis=4)  10.6 us
    sub x3, other arithmetic, advance(): return center + diffusivity * spread - carried  8.86 us
    ppermute x4, starting transfers between devices, with_halo(): lax.ppermute(head, axis, [((i + 1) % count, i) for i in range(ends)])  5.16 us
    ppermute x4, waiting for transfers between devices, with_halo(): lax.ppermute(tail, axis, [(i, (i + 1) % count) for i in range(ends)])  4.83 us
    dot_general x1, matrix products, react(): jnp.einsum('rs,ksc->krc', rate_matrix, mixed, precision=lax.Precision.HIG...  4.44 us
  transfers between devices with their start and end apart: 9, of which 9 were waited for; matrix products, arithmetic and copies ran while one was open for 8% of the time, Pallas kernels for 0%

profile of v1, /device:TPU:0, one launch (start us, length us, event | category | flops | bytes accessed | tf_op | source)
XLA Modules:
  0.0 150.1 jit_solution(9432800274907653215)
XLA Ops:
  6.5 2.4 %fusion.26 = (f32[4,16,1,16,128]{4,3,2,1,0:T(8,128)}, f32[4,16,1,16,128]{4,3,2,1,0:T(8,128)}) fusion(f32[4,16,4,16,128]{4,3,2,1,0:T(8,128)} %param.9), kind=kLoop, calls=%fused_computation.89 | loop fusion | bytes 2097152 | tf_op jit(solution)/shard_map/slice | solution.py:15
  10.3 5.6 %collective-permute-start.1 = (f32[4,16,1,16,128]{4,3,2,1,0:T(8,128)}, f32[4,16,1,16,128]{4,3,2,1,0:T(8,128)S(1)}, u32[]{:S(2)}, u32[]{:S(2)}) collective-permute-start(f32[4,16,1,16,128]{4,3,2,1,0:T(8,128)} %get-tuple-element.49), channel_id=1, source_target_pairs={{0,1},{1,2},{2,3},{4,5},{5,6},{6,7},{8,9},{9,10},{10,11},{12,13},{... | collective-permute-start | bytes 1572872 | tf_op jit(solution)/shard_map/ppermute | solution.py:18
  15.9 2.9 %fusion.27 = (f32[4,16,4,16,127]{4,3,2,1,0:T(8,128)}, f32[4,16,4,16,127]{4,3,2,1,0:T(8,128)}) fusion(f32[4,16,4,16,128]{4,3,2,1,0:T(8,128)S(1)} %copy-done.1), kind=kLoop, calls=%fused_computation.90 | loop fusion | bytes 8323072 | tf_op jit(solution)/shard_map/jit(_roll_static)/slice | solution.py:31
  18.8 2.9 %fusion.28 = (f32[4,16,4,16,1]{4,3,2,1,0:T(8,128)}, f32[4,16,4,16,1]{4,3,2,1,0:T(8,128)}) fusion(f32[4,16,4,16,128]{4,3,2,1,0:T(8,128)S(1)} %copy-done.1), kind=kLoop, calls=%fused_computation.91 | loop fusion | bytes 65536 | tf_op jit(solution)/shard_map/jit(_roll_static)/slice | solution.py:31
  23.7 2.4 %collective-permute-done = f32[4,16,1,16,128]{4,3,2,1,0:T(8,128)S(1)} collective-permute-done((f32[4,16,1,16,128]{4,3,2,1,0:T(8,128)}, f32[4,16,1,16,128]{4,3,2,1,0:T(8,128)S(1)}, u32[]{:S(2)}, u32[]{:S(2)}) %collective-permute-start) | collective-permute-done | bytes 524320 | tf_op jit(solution)/shard_map/ppermute | solution.py:20
  27.3 2.9 %multiply_subtract_fusion.3 = f32[4,16,4,16,128]{4,3,2,1,0:T(8,128)S(1)} fusion(f32[4,16,4,16,128]{4,3,2,1,0:T(8,128)S(1)} %copy-done.1, f32[4,16,4,15,128]{4,3,2,1,0:T(8,128)S(1)} %get-tuple-element.56, f32[4,16,4,1,128]{4,3,2,1,0:T(1,128)S(1)} %get-tuple-element.58, f32[4,16,4,1,128]{4,3,2,1,0:T(1,128)S(1)} %get-tuple-element.57, ...), kind=kLoop, calls=%fused_computation.35 | loop fusion | flops 13107200 | bytes 14057472 | tf_op jit(solution)/shard_map/sub | solution.py:45
  32.1 1.3 collective-permute-start.2
  33.4 4.9 %collective-permute-start.3 = (f32[4,16,1,16,128]{4,3,2,1,0:T(8,128)S(1)}, f32[4,16,1,16,128]{4,3,2,1,0:T(8,128)S(1)}, u32[]{:S(2)}, u32[]{:S(2)}) collective-permute-start(f32[4,16,1,16,128]{4,3,2,1,0:T(8,128)S(1)} %get-tuple-element.39), channel_id=1, source_target_pairs={{0,1},{1,2},{2,3},{4,5},{5,6},{6,7},{8,9},{9,10},{10,11},{12,13},{... | collective-permute-start | bytes 1572872 | tf_op jit(solution)/shard_map/ppermute | solution.py:18
  39.2 8.2 %collective-permute-done.2 = f32[4,16,1,16,128]{4,3,2,1,0:T(8,128)S(1)} collective-permute-done((f32[4,16,1,16,128]{4,3,2,1,0:T(8,128)S(1)}, f32[4,16,1,16,128]{4,3,2,1,0:T(8,128)S(1)}, u32[]{:S(2)}, u32[]{:S(2)}) %collective-permute-start.2) | collective-permute-done | bytes 524320 | tf_op jit(solution)/shard_map/ppermute | solution.py:20
  48.6 3.0 %multiply_subtract_fusion.2 = f32[4,16,4,16,128]{4,3,2,1,0:T(8,128)S(1)} fusion(f32[4,16,4,16,128]{4,3,2,1,0:T(8,128)S(1)} %multiply_subtract_fusion.3, f32[4,16,4,15,128]{4,3,2,1,0:T(8,128)S(1)} %get-tuple-element.46, f32[4,16,4,1,128]{4,3,2,1,0:T(1,128)S(1)} %get-tuple-element.48, f32[4,16,4,1,128]{4,3,2,1,0:T(1,128)S(1)} %get-tuple-element.47, ...), kind=kLoop, calls=%fused_computation.34 | loop fusion | flops 13107200 | bytes 14057472 | tf_op jit(solution)/shard_map/sub | solution.py:45
  53.4 1.3 collective-permute-start.4
  54.7 5.2 %collective-permute-start.5 = (f32[4,16,1,16,128]{4,3,2,1,0:T(8,128)S(1)}, f32[4,16,1,16,128]{4,3,2,1,0:T(8,128)S(1)}, u32[]{:S(2)}, u32[]{:S(2)}) collective-permute-start(f32[4,16,1,16,128]{4,3,2,1,0:T(8,128)S(1)} %get-tuple-element.29), channel_id=1, source_target_pairs={{0,1},{1,2},{2,3},{4,5},{5,6},{6,7},{8,9},{9,10},{10,11},{12,13},{... | collective-permute-start | bytes 1572872 | tf_op jit(solution)/shard_map/ppermute | solution.py:18
  60.8 7.2 %collective-permute-done.4 = f32[4,16,1,16,128]{4,3,2,1,0:T(8,128)S(1)} collective-permute-done((f32[4,16,1,16,128]{4,3,2,1,0:T(8,128)S(1)}, f32[4,16,1,16,128]{4,3,2,1,0:T(8,128)S(1)}, u32[]{:S(2)}, u32[]{:S(2)}) %collective-permute-start.4) | collective-permute-done | bytes 524320 | tf_op jit(solution)/shard_map/ppermute | solution.py:20
  69.2 2.9 %multiply_subtract_fusion.1 = f32[4,16,4,16,128]{4,3,2,1,0:T(8,128)S(1)} fusion(f32[4,16,4,16,128]{4,3,2,1,0:T(8,128)S(1)} %multiply_subtract_fusion.2, f32[4,16,4,15,128]{4,3,2,1,0:T(8,128)S(1)} %get-tuple-element.36, f32[4,16,4,1,128]{4,3,2,1,0:T(1,128)S(1)} %get-tuple-element.38, f32[4,16,4,1,128]{4,3,2,1,0:T(1,128)S(1)} %get-tuple-element.37, ...), kind=kLoop, calls=%fused_computation.33 | loop fusion | flops 13107200 | bytes 14057472 | tf_op jit(solution)/shard_map/sub | solution.py:45
  73.8 1.3 collective-permute-start.6
  75.1 5.0 %collective-permute-start.7 = (f32[4,16,1,16,128]{4,3,2,1,0:T(8,128)S(1)}, f32[4,16,1,16,128]{4,3,2,1,0:T(8,128)S(1)}, u32[]{:S(2)}, u32[]{:S(2)}) collective-permute-start(f32[4,16,1,16,128]{4,3,2,1,0:T(8,128)S(1)} %get-tuple-element.20), channel_id=1, source_target_pairs={{0,1},{1,2},{2,3},{4,5},{5,6},{6,7},{8,9},{9,10},{10,11},{12,13},{... | collective-permute-start | bytes 1572872 | tf_op jit(solution)/shard_map/ppermute | solution.py:18
  80.8 6.7 %collective-permute-done.6 = f32[4,16,1,16,128]{4,3,2,1,0:T(8,128)S(1)} collective-permute-done((f32[4,16,1,16,128]{4,3,2,1,0:T(8,128)S(1)}, f32[4,16,1,16,128]{4,3,2,1,0:T(8,128)S(1)}, u32[]{:S(2)}, u32[]{:S(2)}) %collective-permute-start.6) | collective-permute-done | bytes 524320 | tf_op jit(solution)/shard_map/ppermute | solution.py:20
  88.7 3.9 %fusion.10 = (f32[16,4,16,128]{3,2,1,0:T(8,128)S(1)}, f32[4,16,4,16,128]{4,3,2,1,0:T(8,128)}) fusion(f32[4,4,16,128]{3,2,1,0:T(8,128)S(1)} %get-tuple-element.79, f32[4,4,16,128]{3,2,1,0:T(8,128)S(1)} %get-tuple-element.75, f32[4,4,16,128]{3,2,1,0:T(8,128)S(1)} %get-tuple-element.64, f32[4,16,4,16,128]{4,3,2,1,0:T(8,128)S(1)} %multiply_subtract_fusion.1, ...), kind=kLoop, calls=%fused_computation.73 | loop fusion | flops 13500416 | bytes 14581760 | tf_op jit(solution)/shard_map/reduce_sum | solution.py:67
  93.7 1.8 %reshape.153 = f32[4,16,8192]{2,1,0:T(8,128)S(1)} reshape(f32[4,16,4,16,128]{4,3,2,1,0:T(8,128)} %get-tuple-element.18) | data formatting | bytes 4194304 | tf_op jit(solution)/shard_map/reshape | solution.py:66
  95.5 36.3 %all-gather.2.cloned.1.call-done = f32[8,16,8192]{2,1,0:T(8,128)} async-done(((f32[1,16,8192]{2,1,0:T(8,128)}), f32[8,16,8192]{2,1,0:T(8,128)}) %all-gather.2.cloned.1.call-update) | async-done | bytes 4194320 | tf_op jit(solution)/shard_map/all_gather | solution.py:67
  131.8 2.5 %reduce_sum.19 = f32[16,8192]{1,0:T(8,128)S(1)} reduce(f32[8,16,8192]{2,1,0:T(8,128)} %all-gather.2.cloned.1.call-done, f32[]{:T(128)} %constant.2.clone.1), dimensions={0}, to_apply=%region_1.2 | reduce | flops 917504 | bytes 4718596 | tf_op jit(solution)/shard_map/reduce_sum | solution.py:67
  134.4 4.4 %fusion.3 = f32[4,32,8192]{2,1,0:T(8,128)S(1)} fusion(f32[32]{0:T(128)S(1)} %copy-done.12, f32[4,16,8192]{2,1,0:T(8,128)S(1)} %reshape.153, f32[16,8192]{1,0:T(8,128)S(1)} %broadcast_multiply_fusion, f32[16,8192]{1,0:T(8,128)S(1)} %broadcast_multiply_fusion.1, f32[8192]{0:T(1024)S(1)} %bitcast.34, f32[32,16]{0,1:T(8,128)S(1)} %copy-done), kind=kOutput, calls=%fused_computation.4 | convolution fusion | flops 205520896 | bytes 7374976 | tf_op jit(solution)/shard_map/rs,ksc->krc/dot_general | solution.py:52
  138.8 2.7 %fusion.4 = f32[4,16,8192]{2,1,0:T(8,128)S(1)} fusion(f32[4,32,8192]{2,1,0:T(8,128)S(1)} %fusion.3, f32[4,16,8192]{2,1,0:T(8,128)S(1)} %reshape.153, f32[16,8192]{1,0:T(8,128)S(1)} %broadcast_multiply_fusion, f32[16,8192]{1,0:T(8,128)S(1)} %broadcast_multiply_fusion.1, f32[8192]{0:T(1024)S(1)} %bitcast.35, f32[16,32]{1,0:T(8,128)S(1)} %copy-done.11), kind=kOutput, calls=%fused_computation.6 | convolution fusion | flops 203948032 | bytes 9472000 | tf_op jit(solution)/shard_map/sr,krc->ksc/dot_general | solution.py:54
  141.5 1.7 %copy.22 = f32[8,8,64,128]{3,2,1,0:T(8,128)} copy(f32[8,8,64,128]{3,1,2,0:T(8,128)S(1)} %bitcast.33) | data formatting | bytes 4194304
  (65 shorter events, 16.8 us)
Async XLA Ops:
  6.5 127.8 %copy-start = (f32[32,16]{0,1:T(8,128)S(1)}, f32[32,16]{0,1:T(8,128)}, u32[]{:S(2)}) copy-start(f32[32,16]{0,1:T(8,128)} %param.15) | copy-start | bytes 6148
  6.5 9.4 %copy-start.1 = (f32[4,16,4,16,128]{4,3,2,1,0:T(8,128)S(1)}, f32[4,16,4,16,128]{4,3,2,1,0:T(8,128)}, u32[]{:S(2)}) copy-start(f32[4,16,4,16,128]{4,3,2,1,0:T(8,128)} %param.9) | copy-start | bytes 6291460
  6.5 125.3 %all-gather.2.cloned.1.call-start = ((), (), s32[]{:S(2)}) async-start(), calls=%async_computation | async-start | bytes 4718592 | tf_op jit(solution)/shard_map/all_gather | solution.py:67
  9.0 17.1 %collective-permute-start = (f32[4,16,1,16,128]{4,3,2,1,0:T(8,128)}, f32[4,16,1,16,128]{4,3,2,1,0:T(8,128)S(1)}, u32[]{:S(2)}, u32[]{:S(2)}) collective-permute-start(f32[4,16,1,16,128]{4,3,2,1,0:T(8,128)} %get-tuple-element.50), channel_id=1, source_target_pairs={{1,0},{2,1},{3,2},{5,4},{6,5},{7,6},{9,8},{10,9},{11,10},{13,12},{... | collective-permute-start | bytes 1572872 | tf_op jit(solution)/shard_map/ppermute | solution.py:20
  10.3 17.1 %collective-permute-start.1 = (f32[4,16,1,16,128]{4,3,2,1,0:T(8,128)}, f32[4,16,1,16,128]{4,3,2,1,0:T(8,128)S(1)}, u32[]{:S(2)}, u32[]{:S(2)}) collective-permute-start(f32[4,16,1,16,128]{4,3,2,1,0:T(8,128)} %get-tuple-element.49), channel_id=1, source_target_pairs={{0,1},{1,2},{2,3},{4,5},{5,6},{6,7},{8,9},{9,10},{10,11},{12,13},{... | collective-permute-start | bytes 1572872 | tf_op jit(solution)/shard_map/ppermute | solution.py:18
  18.8 2.9 %copy-start.8 = (f32[4,4,3]{1,0,2:T(4,128)S(1)}, f32[4,4,3]{1,0,2:T(4,128)}, u32[]{:S(2)}) copy-start(f32[4,4,3]{1,0,2:T(4,128)} %param.12) | copy-start | bytes 580
  18.8 3.4 %copy-start.7 = (f32[3,4,16,128]{3,2,1,0:T(8,128)S(1)}, f32[3,4,16,128]{3,2,1,0:T(8,128)}, u32[]{:S(2)}) copy-start(f32[3,4,16,128]{3,2,1,0:T(8,128)} %param.10) | copy-start | bytes 294916
  18.8 3.4 %copy-start.6 = (f32[4,16,128]{2,1,0:T(8,128)S(1)}, f32[4,16,128]{2,1,0:T(8,128)}, u32[]{:S(2)}) copy-start(f32[4,16,128]{2,1,0:T(8,128)} %param.11) | copy-start | bytes 98308
  23.1 4.2 %copy-start.2 = (f32[4,16,4,16,127]{4,3,2,1,0:T(8,128)S(1)}, f32[4,16,4,16,127]{4,3,2,1,0:T(8,128)}, u32[]{:S(2)}) copy-start(f32[4,16,4,16,127]{4,3,2,1,0:T(8,128)} %get-tuple-element.51) | copy-start | bytes 6242308
  23.1 4.2 %copy-start.3 = (f32[4,16,4,16,127]{4,3,2,1,0:T(8,128)S(1)}, f32[4,16,4,16,127]{4,3,2,1,0:T(8,128)}, u32[]{:S(2)}) copy-start(f32[4,16,4,16,127]{4,3,2,1,0:T(8,128)} %get-tuple-element.52) | copy-start | bytes 6242308
  23.1 4.2 %copy-start.4 = (f32[4,16,4,16,1]{4,3,2,1,0:T(8,128)S(1)}, f32[4,16,4,16,1]{4,3,2,1,0:T(8,128)}, u32[]{:S(2)}) copy-start(f32[4,16,4,16,1]{4,3,2,1,0:T(8,128)} %get-tuple-element.53) | copy-start | bytes 49156
  23.2 4.2 %copy-start.5 = (f32[4,16,4,16,1]{4,3,2,1,0:T(8,128)S(1)}, f32[4,16,4,16,1]{4,3,2,1,0:T(8,128)}, u32[]{:S(2)}) copy-start(f32[4,16,4,16,1]{4,3,2,1,0:T(8,128)} %get-tuple-element.54) | copy-start | bytes 49156
  32.1 15.4 %collective-permute-start.2 = (f32[4,16,1,16,128]{4,3,2,1,0:T(8,128)S(1)}, f32[4,16,1,16,128]{4,3,2,1,0:T(8,128)S(1)}, u32[]{:S(2)}, u32[]{:S(2)}) collective-permute-start(f32[4,16,1,16,128]{4,3,2,1,0:T(8,128)S(1)} %get-tuple-element.40), channel_id=1, source_target_pairs={{1,0},{2,1},{3,2},{5,4},{6,5},{7,6},{9,8},{10,9},{11,10},{13,12},{... | collective-permute-start | bytes 1572872 | tf_op jit(solution)/shard_map/ppermute | solution.py:20
  33.4 15.2 %collective-permute-start.3 = (f32[4,16,1,16,128]{4,3,2,1,0:T(8,128)S(1)}, f32[4,16,1,16,128]{4,3,2,1,0:T(8,128)S(1)}, u32[]{:S(2)}, u32[]{:S(2)}) collective-permute-start(f32[4,16,1,16,128]{4,3,2,1,0:T(8,128)S(1)} %get-tuple-element.39), channel_id=1, source_target_pairs={{0,1},{1,2},{2,3},{4,5},{5,6},{6,7},{8,9},{9,10},{10,11},{12,13},{... | collective-permute-start | bytes 1572872 | tf_op jit(solution)/shard_map/ppermute | solution.py:18
  53.4 14.6 %collective-permute-start.4 = (f32[4,16,1,16,128]{4,3,2,1,0:T(8,128)S(1)}, f32[4,16,1,16,128]{4,3,2,1,0:T(8,128)S(1)}, u32[]{:S(2)}, u32[]{:S(2)}) collective-permute-start(f32[4,16,1,16,128]{4,3,2,1,0:T(8,128)S(1)} %get-tuple-element.30), channel_id=1, source_target_pairs={{1,0},{2,1},{3,2},{5,4},{6,5},{7,6},{9,8},{10,9},{11,10},{13,12},{... | collective-permute-start | bytes 1572872 | tf_op jit(solution)/shard_map/ppermute | solution.py:20
  54.7 14.5 %collective-permute-start.5 = (f32[4,16,1,16,128]{4,3,2,1,0:T(8,128)S(1)}, f32[4,16,1,16,128]{4,3,2,1,0:T(8,128)S(1)}, u32[]{:S(2)}, u32[]{:S(2)}) collective-permute-start(f32[4,16,1,16,128]{4,3,2,1,0:T(8,128)S(1)} %get-tuple-element.29), channel_id=1, source_target_pairs={{0,1},{1,2},{2,3},{4,5},{5,6},{6,7},{8,9},{9,10},{10,11},{12,13},{... | collective-permute-start | bytes 1572872 | tf_op jit(solution)/shard_map/ppermute | solution.py:18
  73.8 13.7 %collective-permute-start.6 = (f32[4,16,1,16,128]{4,3,2,1,0:T(8,128)S(1)}, f32[4,16,1,16,128]{4,3,2,1,0:T(8,128)S(1)}, u32[]{:S(2)}, u32[]{:S(2)}) collective-permute-start(f32[4,16,1,16,128]{4,3,2,1,0:T(8,128)S(1)} %get-tuple-element.19), channel_id=1, source_target_pairs={{1,0},{2,1},{3,2},{5,4},{6,5},{7,6},{9,8},{10,9},{11,10},{13,12},{... | collective-permute-start | bytes 1572872 | tf_op jit(solution)/shard_map/ppermute | solution.py:20
  75.1 13.6 %collective-permute-start.7 = (f32[4,16,1,16,128]{4,3,2,1,0:T(8,128)S(1)}, f32[4,16,1,16,128]{4,3,2,1,0:T(8,128)S(1)}, u32[]{:S(2)}, u32[]{:S(2)}) collective-permute-start(f32[4,16,1,16,128]{4,3,2,1,0:T(8,128)S(1)} %get-tuple-element.20), channel_id=1, source_target_pairs={{0,1},{1,2},{2,3},{4,5},{5,6},{6,7},{8,9},{9,10},{10,11},{12,13},{... | collective-permute-start | bytes 1572872 | tf_op jit(solution)/shard_map/ppermute | solution.py:18
  88.7 4.9 %copy-start.10 = (f32[4,16,128]{2,1,0:T(8,128)S(1)}, f32[4,16,128]{2,1,0:T(8,128)}, u32[]{:S(2)}) copy-start(f32[4,16,128]{2,1,0:T(8,128)} %param.13) | copy-start | bytes 98308
  88.7 4.9 %copy-start.9 = (f32[4,16,128]{2,1,0:T(8,128)S(1)}, f32[4,16,128]{2,1,0:T(8,128)}, u32[]{:S(2)}) copy-start(f32[4,16,128]{2,1,0:T(8,128)} %param.14) | copy-start | bytes 98308
  95.5 38.9 %copy-start.12 = (f32[32]{0:T(128)S(1)}, f32[32]{0:T(128)}, u32[]{:S(2)}) copy-start(f32[32]{0:T(128)} %param.17) | copy-start | bytes 388
  134.4 4.5 %copy-start.11 = (f32[16,32]{1,0:T(8,128)S(1)}, f32[16,32]{1,0:T(8,128)}, u32[]{:S(2)}) copy-start(f32[16,32]{1,0:T(8,128)} %param.16) | copy-start | bytes 6148
Sparse Core Ops, SparseCore 0:
  93.7 38.1 all-gather.1
